TPU v7x, 32 devices: a whole 2x2x4 slice. The times are simulated.
32 devices in a mesh: groups: 2 (over y), expert: 8 (over z, core), dp: 2 (over x).
Axes of the slice: x: 2, y: 2, z: 4, core: 2. Of those that a mesh axis runs over, the one named last changes fastest.
Arguments:
- tokens: bfloat16 [1024, 2048], P(('groups', 'expert'), 'dp'), parts along dimension 0, may hold values from -6 to 6
- expert_ids: int32 [1024, 8], P(('groups', 'expert')), parts along dimension 0, may hold values from 0 to 15, all different within a row; in each aligned block of 64 rows (0 to 63, 64 to 127, ...) at most 64 rows name the same one
- gate_levels: int32 [1024, 8], P(('groups', 'expert')), parts along dimension 0, may hold values from 1 to 255
- gate_weight: bfloat16 [16, 2048, 1536], P('expert', None, 'dp'), may hold values from -0.125 to 0.125
- up_weight: bfloat16 [16, 2048, 1536], P('expert', None, 'dp'), may hold values from -0.125 to 0.125
- down_weight: bfloat16 [16, 1536, 2048], P('expert', None, 'dp'), may hold values from -0.15625 to 0.15625
Outputs:
- mixed: bfloat16 [1024, 2048], P(('groups', 'expert'), 'dp'), parts along dimension 0
There are 2 independent parts, one for each index of `groups`. A program takes and returns all parts, laid end to end along the dimension named above; an argument that names none is the same for every part. Nothing has to cross between parts.
Inputs may be any that keep to these rules, and one draw needn't show every extreme that they name: `expert_ids`: each row names 8 different experts. Among the rows of one index of the expert axis no expert is named more than 64 times, a bound that some block reaches.
All inputs are finite; a program needn't handle non-finite values.
Results may differ from a plain program's by a relative error of at most 0.0057.
Values may be sent and summed in bfloat16 or wider, within the bound.
A program may use at most 64 MiB of HBM per device.

v0:
```python
import jax
import jax.numpy as jnp
from jax import lax
from jax.sharding import PartitionSpec as P


def slot_numbers(chosen_ids, experts, capacity):
    flat_ids = chosen_ids.reshape(-1)
    labels = jnp.arange(experts, dtype=jnp.int32)
    onehot = (flat_ids[:, None] == labels[None, :]).astype(jnp.int32)
    before = jnp.cumsum(onehot, axis=0) - onehot
    position = jnp.sum(before * onehot, axis=1)
    return (flat_ids * capacity + position).reshape(chosen_ids.shape)


def route_matrix(slots, count):
    targets = jnp.arange(count, dtype=jnp.int32)
    return jnp.any(targets[:, None, None] == slots[None, :, :], axis=2).astype(jnp.bfloat16)


def on_device(tokens, expert_ids, gate_levels, gate_weight, up_weight, down_weight):
    tok_dev = tokens.shape[0]
    picks = expert_ids.shape[1]
    exp_dev = gate_weight.shape[0]
    n_expert = lax.axis_size("expert")
    experts = exp_dev * n_expert
    capacity = min(tok_dev, max(2, 2 * tok_dev * picks // experts))
    slot_count = experts * capacity
    own_slots = slot_numbers(expert_ids, experts, capacity)
    route = route_matrix(own_slots, slot_count)
    whole = lax.all_gather(tokens, "dp", axis=1, tiled=True)
    outgoing = jnp.dot(route, whole, preferred_element_type=jnp.float32).astype(jnp.bfloat16)
    outgoing = outgoing.reshape(n_expert, exp_dev, capacity, whole.shape[1])
    arrived = lax.all_to_all(outgoing, "expert", split_axis=0, concat_axis=0, tiled=True)
    gate_part = jnp.einsum(
        "sxcd,xdf->sxcf", arrived, gate_weight, preferred_element_type=jnp.float32
    )
    up_part = jnp.einsum("sxcd,xdf->sxcf", arrived, up_weight, preferred_element_type=jnp.float32)
    hidden = (jax.nn.silu(gate_part) * up_part).astype(jnp.bfloat16)
    out_features = down_weight.shape[2]
    outputs = jnp.einsum(
        "sxcf,xfk->sxck",
        lax.all_gather(hidden, "dp", axis=3, tiled=True),
        down_weight,
        preferred_element_type=jnp.float32,
    )
    result = outputs.astype(jnp.bfloat16)
    returned = lax.all_to_all(result, "expert", split_axis=0, concat_axis=0, tiled=True)
    returned = returned.reshape(slot_count, out_features)
    shares = gate_levels.astype(jnp.float32) / 256.0
    targets = jnp.arange(slot_count, dtype=jnp.int32)
    weighting = jnp.sum(
        jnp.where(
            targets[None, :, None] == own_slots[:, None, :], shares[:, None, :], jnp.float32(0.0)
        ),
        axis=2,
    )
    weighting = weighting.astype(jnp.bfloat16)
    combined = jnp.dot(weighting, returned, preferred_element_type=jnp.float32)
    return combined.astype(jnp.bfloat16)


def solution(mesh):
    in_specs = (
        P(("groups", "expert"), "dp"),
        P(("groups", "expert"), None),
        P(("groups", "expert"), None),
        P("expert", None, "dp"),
        P("expert", None, "dp"),
        P("expert", None, "dp"),
    )
    out_specs = P(("groups", "expert"), "dp")
    return jax.shard_map(
        on_device, mesh=mesh, in_specs=in_specs, out_specs=out_specs, check_vma=False
    )
```

profile of v0, /device:TPU:0, one launch (start us, length us, event | category | flops | bytes accessed | tf_op | source)
XLA Modules:
  0.0 241.4 jit_solution(17744205040662272902)
XLA Ops:
  6.5 0.0 all-gather.2.cloned.1.call-start
  6.5 0.8 copy.37
  7.3 0.1 eq.56
  7.4 0.1 eq.52
  7.5 1.2 reduce-window.6
  8.7 0.2 slice_reduce_fusion
  8.9 0.1 fusion.22
  9.0 0.1 reduce_sum.21
  9.1 0.1 copy.40
  9.2 0.7 multiply_add_fusion
  9.9 0.1 copy.41
  10.0 0.7 fusion.12
  10.7 7.4 %all_gather.6 = bf16[64,2048]{1,0:T(8,128)(2,1)S(1)} all-gather(bf16[64,1024]{1,0:T(8,128)(2,1)} %param.6), channel_id=1, replica_groups=mesh['groups'=2,'expert'=8,'dp'=2] {'dp'}, dimensions={1}, use_global_device_ids=true | all-gather | bytes 393216 | tf_op jit(solution)/shard_map/all_gather | solution.py:31
  18.1 0.0 slice-start
  18.1 1.3 convolution_convert_fusion
  19.4 0.0 slice-start.1
  19.4 0.0 slice-start.2
  19.4 99.1 %all_to_all.10 = bf16[8,2,64,2048]{3,2,1,0:T(8,128)(2,1)S(1)} all-to-all(bf16[8,2,64,2048]{3,2,1,0:T(8,128)(2,1)S(1)} %bitcast.64), channel_id=1, replica_groups=mesh['groups'=2,'expert'=8,'dp'=2] {'expert'}, dimensions={0} | all-to-all | bytes 8388608 | tf_op jit(solution)/shard_map/all_to_all | solution.py:34
  118.5 0.0 slice-done
  118.5 0.0 slice-done.1
  118.5 0.0 slice-start.3
  118.5 3.5 %fusion.2 = f32[2,8,64,768]{3,2,1,0:T(8,128)S(1)} fusion(bf16[2,2048,768]{2,1,0:T(8,128)(2,1)S(1)} %bitcast.67, bf16[8,2,64,2048]{3,2,1,0:T(8,128)(2,1)S(1)} %all_to_all.10), kind=kOutput, calls=%fused_computation.2 | convolution fusion | flops 3221225472 | bytes 13631488 | tf_op jit(solution)/shard_map/sxcd,xdf->sxcf/dot_general | solution.py:38
  122.0 0.0 slice-done.2
  122.0 0.0 slice-done.3
  122.0 4.9 %fusion.8 = bf16[8,2,64,768]{3,2,0,1:T(8,128)(2,1)} fusion(f32[2,8,64,768]{3,2,1,0:T(8,128)S(1)} %fusion.2, bf16[2,2048,768]{2,1,0:T(8,128)(2,1)S(1)} %bitcast.69, bf16[8,2,64,2048]{3,2,1,0:T(8,128)(2,1)S(1)} %all_to_all.10), kind=kOutput, calls=%fused_computation.10 | convolution fusion | flops 3225944064 | bytes 15204352 | tf_op jit(solution)/shard_map/sxcd,xdf->sxcf/dot_general | solution.py:35
  126.9 0.0 all-gather.2.cloned.1.call-update
  126.9 44.0 %all-gather.2.cloned.1.call-done = bf16[8,2,64,1536]{3,2,0,1:T(8,128)(2,1)} async-done(((bf16[8,2,64,768]{3,2,0,1:T(8,128)(2,1)}), bf16[8,2,64,1536]{3,2,0,1:T(8,128)(2,1)}) %all-gather.2.cloned.1.call-update) | async-done | bytes 3145744 | tf_op jit(solution)/shard_map/all_gather | solution.py:43
  170.9 7.2 %convert_bitcast_fusion = bf16[8,2,64,1024]{3,2,0,1:T(8,128)(2,1)S(1)} fusion(bf16[8,2,64,1536]{3,2,0,1:T(8,128)(2,1)} %all-gather.2.cloned.1.call-done, bf16[2,1536,1024]{2,1,0:T(8,128)(2,1)} %param.11), kind=kOutput, calls=%fused_computation.16 | convolution fusion | flops 3222274048 | bytes 11534336 | tf_op jit(solution)/shard_map/sxcf,xfk->sxck/dot_general | solution.py:41
  178.1 1.6 copy.46
  179.6 0.0 copy-start
  179.6 4.7 %all-to-all-start.1 = ((bf16[8,2,64,1024]{3,2,1,0:T(8,128)(2,1)}), bf16[8,2,64,1024]{3,2,1,0:T(8,128)(2,1)S(1)}, u32[]{:S(2)}, u32[]{:S(2)}) async-start(bf16[8,2,64,1024]{3,2,1,0:T(8,128)(2,1)} %copy.46), calls=%async_computation.1 | async-start | bytes 4194304 | tf_op jit(solution)/shard_map/all_to_all | solution.py:48
  184.4 0.0 copy-done
  184.4 0.1 copy.42
  184.5 0.7 select_reduce_fusion
  185.2 48.2 %all-to-all-done.1 = bf16[8,2,64,1024]{3,2,1,0:T(8,128)(2,1)S(1)} async-done(((bf16[8,2,64,1024]{3,2,1,0:T(8,128)(2,1)}), bf16[8,2,64,1024]{3,2,1,0:T(8,128)(2,1)S(1)}, u32[]{:S(2)}, u32[]{:S(2)}) %all-to-all-start.1) | async-done | bytes 2097184 | tf_op jit(solution)/shard_map/all_to_all | solution.py:48
  233.4 1.1 convolution_convert_fusion.1
  (6 shorter events, 0.1 us)
Async XLA Ops:
  6.5 164.4 %all-gather.2.cloned.1.call-start = ((), (), s32[]{:S(2)}) async-start(), calls=%async_computation.2 | async-start | bytes 4718592 | tf_op jit(solution)/shard_map/all_gather | solution.py:43
  18.1 100.4 %slice-start = ((s8[6291456]{0:T(1024)(128)(4,1)}), s8[4194304]{0:T(1024)(128)(4,1)S(1)}, s32[]{:S(2)}) async-start(s8[6291456]{0:T(1024)(128)(4,1)} %bitcast.66), calls=%async_computation.3 | async-start | bytes 8388608
  19.4 99.1 %slice-start.1 = ((s8[6291456]{0:T(1024)(128)(4,1)}), s8[2097152]{0:T(1024)(128)(4,1)S(1)}, s32[]{:S(2)}) async-start(s8[6291456]{0:T(1024)(128)(4,1)} %bitcast.66), calls=%async_computation.4 | async-start | bytes 4194304
  19.4 102.6 %slice-start.2 = ((s8[6291456]{0:T(1024)(128)(4,1)}), s8[4194304]{0:T(1024)(128)(4,1)S(1)}, s32[]{:S(2)}) async-start(s8[6291456]{0:T(1024)(128)(4,1)} %bitcast.68), calls=%async_computation.5 | async-start | bytes 8388608
  118.5 3.5 %slice-start.3 = ((s8[6291456]{0:T(1024)(128)(4,1)}), s8[2097152]{0:T(1024)(128)(4,1)S(1)}, s32[]{:S(2)}) async-start(s8[6291456]{0:T(1024)(128)(4,1)} %bitcast.68), calls=%async_computation.6 | async-start | bytes 4194304
  179.6 4.7 %copy-start = (s32[64,8]{0,1:T(8,128)S(1)}, s32[64,8]{0,1:T(8,128)}, u32[]{:S(2)}) copy-start(s32[64,8]{0,1:T(8,128)} %param.8) | copy-start | bytes 6148
  179.6 53.8 %all-to-all-start.1 = ((bf16[8,2,64,1024]{3,2,1,0:T(8,128)(2,1)}), bf16[8,2,64,1024]{3,2,1,0:T(8,128)(2,1)S(1)}, u32[]{:S(2)}, u32[]{:S(2)}) async-start(bf16[8,2,64,1024]{3,2,1,0:T(8,128)(2,1)} %copy.46), calls=%async_computation.1 | async-start | bytes 4194304 | tf_op jit(solution)/shard_map/all_to_all | solution.py:48
Sparse Core Ops, SparseCore 0:
  127.0 43.8 all-gather.1
where the time goes:
time: 242 us; the launch traced here: 241 us
  blocking collectives  107 us (44%)
  waiting for transfers between devices  92.2 us (38%)
  matrix products  17.9 us (7%)
  between operations  13.5 us (6%)
  starting transfers between devices  4.74 us (2%)
  other arithmetic  3.42 us (1%)
  local copies, waits for them, and re-layouts  3.08 us (1%)
    all_to_all x1, blocking collectives, on_device(): lax.all_to_all(outgoing, 'expert', split_axis=0, concat_axis=0, tiled=True)  99.1 us
    all_to_all x1, waiting for transfers between devices, on_device(): lax.all_to_all(result, 'expert', split_axis=0, concat_axis=0, tiled=True)  48.2 us
    all_gather x1, waiting for transfers between devices, on_device(): lax.all_gather(hidden, 'dp', axis=3, tiled=True)  44 us
    all_gather x1, blocking collectives, on_device(): whole = lax.all_gather(tokens, 'dp', axis=1, tiled=True)  7.39 us
    dot_general x1, matrix products, on_device(): jnp.einsum('sxcf,xfk->sxck', lax.all_gather(hidden, 'dp', axis=3, tiled=T...  7.15 us
    dot_general x1, matrix products, on_device(): jnp.einsum('sxcd,xdf->sxcf', arrived, gate_weight, preferred_element_type...  4.87 us
  transfers between devices with their start and end apart: 2, of which 2 were waited for; matrix products, arithmetic and copies ran while one was open for 0% of the time, Pallas kernels for 0%

commit v1 on v0

--- a/solution.py
+++ b/solution.py
@@ -1,7 +1,14 @@
+import functools
+
 import jax
 import jax.numpy as jnp
 from jax import lax
+from jax.experimental import pallas as pl
+from jax.experimental.pallas import tpu as pltpu
 from jax.sharding import PartitionSpec as P
+
+MESH = pl.DeviceIdType.MESH
+WIDE = 256
 
 
 def slot_numbers(chosen_ids, experts, capacity):
@@ -18,7 +25,7 @@
     return jnp.any(targets[:, None, None] == slots[None, :, :], axis=2).astype(jnp.bfloat16)
 
 
-def on_device(tokens, expert_ids, gate_levels, gate_weight, up_weight, down_weight):
+def routed_on_device(tokens, expert_ids, gate_levels, gate_weight, up_weight, down_weight):
     tok_dev = tokens.shape[0]
     picks = expert_ids.shape[1]
     exp_dev = gate_weight.shape[0]
@@ -60,6 +67,303 @@
     return combined.astype(jnp.bfloat16)
 
 
+def near_first(chips):
+    return [sorted(range(chips), key=lambda q: (abs(q - z), q if 2 * z < chips else -q)) for z in range(chips)]
+
+
+def dense_kernel(
+    chips, tok, ids, levels, gate_hbm, up_hbm, down_hbm, out,
+    gate_w, up_w, down_w, x_buf, s_buf, hid, part, pair_out, pair_in, ret_out, ret_in, total,
+    w_sem, x_send, x_recv, t_send, h_send, h_recv, p_send, p_recv, r_send, r_recv,
+):
+    e = lax.axis_index("expert")
+    d = lax.axis_index("dp")
+    z, c = lax.div(e, 2), lax.rem(e, 2)
+    rows = tok.shape[0]
+    exp_dev, depth, ff = gate_w.shape
+    half = depth // 2
+    width = down_w.shape[2]
+    mate = z * 2 + 1 - c
+
+    loads = []
+    for x in range(exp_dev):
+        for i, (source, held) in enumerate(((gate_hbm, gate_w), (up_hbm, up_w))):
+            loads.append(pltpu.make_async_copy(source.at[x], held.at[x], w_sem.at[x, i]))
+    for x in range(exp_dev):
+        loads.append(pltpu.make_async_copy(down_hbm.at[x], down_w.at[x], w_sem.at[x, 2]))
+    for load in loads:
+        load.start()
+
+    barrier = pltpu.get_barrier_semaphore()
+    pl.semaphore_signal(barrier, inc=1, device_id={"dp": 1 - d}, device_id_type=MESH)
+    pl.semaphore_signal(barrier, inc=1, device_id={"expert": mate}, device_id_type=MESH)
+    for i in range(1, chips):
+        pl.semaphore_signal(
+            barrier, inc=1, device_id={"expert": lax.rem(z + i, chips) * 2 + c}, device_id_type=MESH
+        )
+
+    own_rows = pl.ds(pl.multiple_of(c * rows, rows), rows)
+    lane = lax.broadcasted_iota(jnp.int32, (rows, 128), 1)
+    share = jnp.zeros((rows, 128), jnp.float32)
+    for k in range(ids.shape[1]):
+        level = levels[:, k : k + 1].astype(jnp.float32) / 256.0
+        share = share + jnp.where(ids[:, k : k + 1] == lane, level, 0.0)
+    s_buf[z, own_rows, :] = share.astype(s_buf.dtype)
+    x_buf[z, d, own_rows, :] = tok[...]
+    pl.semaphore_wait(barrier, chips + 1)
+
+    def unit(q, core, j):
+        at = pl.ds(pl.multiple_of(core * rows, rows), rows)
+        if isinstance(j, int) and j == 2:
+            return s_buf.at[q, at]
+        return x_buf.at[q, j, at]
+
+    def swap():
+        return pltpu.make_async_remote_copy(
+            src_ref=tok, dst_ref=unit(z, c, d), send_sem=t_send, recv_sem=x_recv.at[z, c, d],
+            device_id={"dp": 1 - d}, device_id_type=MESH,
+        )
+
+    def forward(q, j, way):
+        target = (mate, e + 2, e - 2)[way]
+        return pltpu.make_async_remote_copy(
+            src_ref=unit(q, c, j), dst_ref=unit(q, c, j),
+            send_sem=x_send.at[q, j, way], recv_sem=x_recv.at[q, c, j],
+            device_id={"expert": target}, device_id_type=MESH,
+        )
+
+    def arrived(q, core, j):
+        pltpu.make_async_remote_copy(
+            src_ref=unit(q, core, j), dst_ref=unit(q, core, j),
+            send_sem=t_send, recv_sem=x_recv.at[q, core, j],
+            device_id={"expert": mate}, device_id_type=MESH,
+        ).wait_recv()
+
+    def send_own(j, finish=False):
+        for way, there in ((0, None), (1, z < chips - 1), (2, z > 0)):
+            def go(way=way):
+                copy = forward(z, j, way)
+                copy.wait_send() if finish else copy.start()
+            go() if there is None else pl.when(there)(go)
+
+    def relay(step, finish=False):
+        for way in (1, 2):
+            q = z - step if way == 1 else z + step
+            inside = z >= step if way == 1 else z + step < chips
+            further = jnp.logical_and(inside, z < chips - 1) if way == 1 else jnp.logical_and(inside, z > 0)
+            for j in (0, 1, 2):
+                @pl.when(inside)
+                def _(q=q, j=j):
+                    if finish:
+                        forward(q, j, 0).wait_send()
+                    else:
+                        arrived(q, c, j)
+
+                @pl.when(further)
+                def _(q=q, j=j, way=way):
+                    copy = forward(q, j, way)
+                    copy.wait_send() if finish else copy.start()
+
+                if not finish:
+                    @pl.when(inside)
+                    def _(q=q, j=j):
+                        forward(q, j, 0).start()
+
+    swap().start()
+    send_own(d)
+    send_own(2)
+    arrived(z, c, 1 - d)
+    send_own(1 - d)
+
+    table = near_first(chips)
+    order = []
+    for step in range(chips):
+        q = jnp.int32(0)
+        for place in range(chips):
+            q = jnp.where(z == place, jnp.int32(table[place][step]), q)
+        order.append(q)
+
+    def cross(step, x):
+        return pltpu.make_async_remote_copy(
+            src_ref=hid.at[step, x, d], dst_ref=hid.at[step, x, d],
+            send_sem=h_send.at[step, x], recv_sem=h_recv.at[step, x],
+            device_id={"dp": 1 - d}, device_id_type=MESH,
+        )
+
+    def crossed(step, x):
+        pltpu.make_async_remote_copy(
+            src_ref=hid.at[step, x, 1 - d], dst_ref=hid.at[step, x, 1 - d],
+            send_sem=h_send.at[step, x], recv_sem=h_recv.at[step, x],
+            device_id={"dp": 1 - d}, device_id_type=MESH,
+        ).wait_recv()
+
+    def units(step):
+        q = order[step]
+        for j in (0, 1, 2):
+            arrived(q, 1 - c, j)
+        for x in range(exp_dev):
+            if step == 0:
+                loads[2 * x].wait()
+                loads[2 * x + 1].wait()
+
+            @pl.loop(0, ff // WIDE)
+            def _(t):
+                cols = pl.ds(pl.multiple_of(t * WIDE, WIDE), WIDE)
+                low, high = x_buf[q, 0], x_buf[q, 1]
+                gate = jnp.dot(low, gate_w[x, :half, cols], preferred_element_type=jnp.float32)
+                gate = gate + jnp.dot(high, gate_w[x, half:, cols], preferred_element_type=jnp.float32)
+                up = jnp.dot(low, up_w[x, :half, cols], preferred_element_type=jnp.float32)
+                up = up + jnp.dot(high, up_w[x, half:, cols], preferred_element_type=jnp.float32)
+                hid[step, x, d, :, cols] = (gate / (1.0 + jnp.exp(-gate)) * up).astype(hid.dtype)
+
+            cross(step, x).start()
+
+    def hand_over(step):
+        return pltpu.make_async_remote_copy(
+            src_ref=pair_out.at[step], dst_ref=pair_in.at[step],
+            send_sem=p_send.at[step], recv_sem=p_recv.at[step],
+            device_id={"expert": mate}, device_id_type=MESH,
+        )
+
+    def give_back(step):
+        return pltpu.make_async_remote_copy(
+            src_ref=ret_out.at[step], dst_ref=ret_in.at[z],
+            send_sem=r_send.at[step], recv_sem=r_recv.at[z],
+            device_id={"expert": order[step] * 2 + c}, device_id_type=MESH,
+        )
+
+    def outputs(step):
+        q = order[step]
+        lanes = lax.broadcasted_iota(jnp.int32, (2 * rows, 128), 1)
+        for x in range(exp_dev):
+            if step == 0:
+                loads[2 * exp_dev + x].wait()
+            picked = jnp.where(lanes == e * exp_dev + x, s_buf[q].astype(jnp.float32), 0.0)
+            weight = jnp.sum(picked, axis=1, keepdims=True)
+            crossed(step, x)
+
+            @pl.loop(0, width // WIDE)
+            def _(t):
+                cols = pl.ds(pl.multiple_of(t * WIDE, WIDE), WIDE)
+                res = jnp.dot(hid[step, x, 0], down_w[x, :ff, cols], preferred_element_type=jnp.float32)
+                res = res + jnp.dot(hid[step, x, 1], down_w[x, ff:, cols], preferred_element_type=jnp.float32)
+                res = res * weight
+                for core in range(2):
+                    piece = res[core * rows : (core + 1) * rows]
+                    if x == 0:
+                        part[core, :, cols] = piece
+                    else:
+                        part[core, :, cols] += piece
+
+        pair_out[step] = part[1 - c].astype(pair_out.dtype)
+        hand_over(step).start()
+        hand_over(step).wait_recv()
+        both = part[c] + pair_in[step].astype(jnp.float32)
+        if step == 0:
+            total[...] = both
+        else:
+            ret_out[step] = both.astype(ret_out.dtype)
+            give_back(step).start()
+
+    units(0)
+    for step in range(1, chips):
+        relay(step)
+        units(step)
+        outputs(step - 1)
+    outputs(chips - 1)
+
+    for i in range(1, chips):
+        q = lax.rem(z + i, chips)
+        pltpu.make_async_remote_copy(
+            src_ref=ret_in.at[q], dst_ref=ret_in.at[q], send_sem=r_send.at[i], recv_sem=r_recv.at[q],
+            device_id={"expert": mate}, device_id_type=MESH,
+        ).wait_recv()
+        if i < chips - 1:
+            total[...] += ret_in[q].astype(jnp.float32)
+        else:
+            out[...] = (total[...] + ret_in[q].astype(jnp.float32)).astype(out.dtype)
+
+    swap().wait_send()
+    for j in (0, 1, 2):
+        send_own(j, finish=True)
+    for step in range(1, chips):
+        relay(step, finish=True)
+        give_back(step).wait_send()
+    for step in range(chips):
+        hand_over(step).wait_send()
+        for x in range(exp_dev):
+            cross(step, x).wait_send()
+
+
+def dense_on_device(tokens, expert_ids, gate_levels, gate_weight, up_weight, down_weight):
+    chips = lax.axis_size("expert") // 2
+    rows, own = tokens.shape
+    exp_dev, depth, ff = gate_weight.shape
+    width = down_weight.shape[2]
+    kind = tokens.dtype
+    vmem = pl.BlockSpec(memory_space=pltpu.VMEM)
+    anywhere = pl.BlockSpec(memory_space=pl.ANY)
+    dma = pltpu.SemaphoreType.DMA
+    flops = 2 * chips * 2 * rows * exp_dev * (2 * depth * ff + 2 * ff * width)
+    return pl.pallas_call(
+        functools.partial(dense_kernel, chips),
+        out_shape=jax.ShapeDtypeStruct((rows, width), kind),
+        in_specs=[vmem, vmem, vmem, anywhere, anywhere, anywhere],
+        out_specs=vmem,
+        scratch_shapes=[
+            pltpu.VMEM(gate_weight.shape, kind),
+            pltpu.VMEM(up_weight.shape, kind),
+            pltpu.VMEM(down_weight.shape, kind),
+            pltpu.VMEM((chips, 2, 2 * rows, own), kind),
+            pltpu.VMEM((chips, 2 * rows, 128), kind),
+            pltpu.VMEM((chips, exp_dev, 2, 2 * rows, ff), kind),
+            pltpu.VMEM((2, rows, width), jnp.float32),
+            pltpu.VMEM((chips, rows, width), kind),
+            pltpu.VMEM((chips, rows, width), kind),
+            pltpu.VMEM((chips, rows, width), kind),
+            pltpu.VMEM((chips, rows, width), kind),
+            pltpu.VMEM((rows, width), jnp.float32),
+            dma((exp_dev, 3)),
+            dma((chips, 3, 3)),
+            dma((chips, 2, 3)),
+            dma,
+            dma((chips, exp_dev)),
+            dma((chips, exp_dev)),
+            dma((chips,)),
+            dma((chips,)),
+            dma((chips,)),
+            dma((chips,)),
+        ],
+        compiler_params=pltpu.CompilerParams(
+            collective_id=0, has_side_effects=True, vmem_limit_bytes=60 * 1024 * 1024
+        ),
+        cost_estimate=pl.CostEstimate(
+            flops=flops, bytes_accessed=2 * 3 * gate_weight.size, transcendentals=0
+        ),
+    )(tokens, expert_ids, gate_levels, gate_weight, up_weight, down_weight)
+
+
+def on_device(tokens, expert_ids, gate_levels, gate_weight, up_weight, down_weight):
+    rows, own = tokens.shape
+    exp_dev, depth, ff = gate_weight.shape
+    n_expert = lax.axis_size("expert")
+    width = down_weight.shape[2]
+    experts = exp_dev * n_expert
+    dense = (
+        2 * rows * expert_ids.shape[1] >= rows * experts
+        and lax.axis_size("dp") == 2
+        and n_expert % 2 == 0
+        and n_expert >= 4
+        and experts <= 128
+        and rows % 16 == 0
+        and own % 128 == 0
+        and ff % WIDE == 0
+        and width % WIDE == 0
+    )
+    call = dense_on_device if dense else routed_on_device
+    return call(tokens, expert_ids, gate_levels, gate_weight, up_weight, down_weight)
+
+
 def solution(mesh):
     in_specs = (
         P(("groups", "expert"), "dp"),

time: 242 us -> 63.1 us (0.26)
  blocking collectives: 107 us -> 0 us
  waiting for transfers between devices: 92.2 us -> 0 us
  Pallas kernels: 0 us -> 58.5 us
  matrix products: 17.9 us -> 0 us
  between operations: 13.5 us -> 0.01 us
  starting transfers between devices: 4.74 us -> 0 us
  other arithmetic: 3.42 us -> 0 us
    all_to_all x1 -> x0, blocking collectives: 99.1 us -> none  [on_device(): lax.all_to_all(outgoing, 'expert', split_axis=0, concat_axis=0, tiled=True)]
    pallas_call x0 -> x1, Pallas kernels: none -> 58.5 us  [dense_on_device(): pl.pallas_call(functools.partial(dense_kernel, chips), out_shape=jax.Shap...]
    all_to_all x1 -> x0, waiting for transfers between devices: 48.2 us -> none  [on_device(): lax.all_to_all(result, 'expert', split_axis=0, concat_axis=0, tiled=True)]
    all_gather x1 -> x0, waiting for transfers between devices: 44 us -> none  [on_device(): lax.all_gather(hidden, 'dp', axis=3, tiled=True)]
    dot_general x5 -> x0, matrix products: 17.9 us -> none  [the longest x1 7.15 us: on_device(): jnp.einsum('sxcf,xfk->sxck', lax.all_gather(hidden, 'dp', axis=3, tiled=T...]
    all_gather x1 -> x0, blocking collectives: 7.39 us -> none  [on_device(): whole = lax.all_gather(tokens, 'dp', axis=1, tiled=True)]
    all_to_all x1 -> x0, starting transfers between devices: 4.74 us -> none  [on_device(): lax.all_to_all(result, 'expert', split_axis=0, concat_axis=0, tiled=True)]
    unnamed x11 -> x3, local copies, waits for them, and re-layouts: 0.8 us -> 4.32 us
  transfers between devices with their start and end apart: 2 -> 0, of which waited for: 2 -> 0; matrix products, arithmetic and copies ran while one was open for 0% -> 0% of each run, Pallas kernels for 0% -> 0%
where the time goes in v1:
time: 63.1 us; the launch traced here: 62.9 us
  Pallas kernels  58.5 us (93%)
  local copies, waits for them, and re-layouts  4.32 us (7%)
    pallas_call x1, Pallas kernels, dense_on_device(): pl.pallas_call(functools.partial(dense_kernel, chips), out_shape=jax.Shap...  58.5 us
    unnamed x3, local copies, waits for them, and re-layouts  4.32 us

profile of v1, /device:TPU:0, one launch (start us, length us, event | category | flops | bytes accessed | tf_op | source)
XLA Modules:
  0.0 62.9 jit_solution(16019238431576957156)
XLA Ops:
  0.0 1.4 %copy.7.ids = s32[64,8]{1,0:T(8,128)} copy(s32[64,8]{0,1:T(8,128)} %param.7) | data formatting | bytes 4096 | tf_op args[1]
  1.4 1.4 %copy.8.levels = s32[64,8]{1,0:T(8,128)} copy(s32[64,8]{0,1:T(8,128)} %param.8) | data formatting | bytes 4096 | tf_op args[2]
  2.8 58.5 %shard_map.64 = bf16[64,1024]{1,0:T(8,128)(2,1)} custom-call(bf16[64,1024]{1,0:T(8,128)(2,1)} %tok.1, s32[64,8]{1,0:T(8,128)} %copy.7.ids, s32[64,8]{1,0:T(8,128)} %copy.8.levels, bf16[2,2048,768]{2,1,0:T(8,128)(2,1)} %gate_hbm.1, bf16[2,2048,768]{2,1,0:T(8,128)(2,1)} %up_hbm.1, bf16[2,1536,1024]{2,1,0:T(8,128)(2,1)} %down_hbm.1), custom_call_target="tpu_custom_call" | custom-call | flops 9663676416 | bytes 18874368 | tf_op jit(solution)/shard_map/pallas_call | solution.py:308
  61.3 1.6 %copy.10 = bf16[64,1024]{1,0:T(8,128)(2,1)} copy(bf16[64,1024]{1,0:T(8,128)(2,1)} %shard_map.64) | data formatting | bytes 262144

commit v2 on v1

--- a/solution.py
+++ b/solution.py
@@ -67,24 +67,51 @@
     return combined.astype(jnp.bfloat16)
 
 
-def near_first(chips):
-    return [sorted(range(chips), key=lambda q: (abs(q - z), q if 2 * z < chips else -q)) for z in range(chips)]
+def visit_order(chips):
+    table = []
+    for z in range(chips):
+        near = sorted(range(chips), key=lambda q: (abs(q - z), q if 2 * z < chips else -q))
+        if 0 < z < chips - 1:
+            near = near[:1] + near[2:] + near[1:2]
+        else:
+            near = near[:-2] + [near[-1], near[-2]]
+        table.append(near)
+    return table
 
 
 def dense_kernel(
-    chips, tok, ids, levels, gate_hbm, up_hbm, down_hbm, out,
-    gate_w, up_w, down_w, x_buf, s_buf, hid, part, pair_out, pair_in, ret_out, ret_in, total,
-    w_sem, x_send, x_recv, t_send, h_send, h_recv, p_send, p_recv, r_send, r_recv,
+    chips, tok_hbm, ids_hbm, levels_hbm, gate_hbm, up_hbm, down_hbm, out,
+    ids, levels, gate_w, up_w, down_w, x_buf, s_buf, hid, part, pair_out, pair_in, ret_out, ret_in, total,
+    i_sem, w_sem, x_send, x_recv, t_send, h_send, h_recv, p_send, p_recv, r_send, r_recv,
 ):
     e = lax.axis_index("expert")
     d = lax.axis_index("dp")
     z, c = lax.div(e, 2), lax.rem(e, 2)
-    rows = tok.shape[0]
+    rows = tok_hbm.shape[0]
     exp_dev, depth, ff = gate_w.shape
     half = depth // 2
     width = down_w.shape[2]
     mate = z * 2 + 1 - c
 
+    barrier = pltpu.get_barrier_semaphore()
+    pl.semaphore_signal(barrier, inc=1, device_id={"dp": 1 - d}, device_id_type=MESH)
+    pl.semaphore_signal(barrier, inc=1, device_id={"expert": mate}, device_id_type=MESH)
+
+    @pl.when(z > 0)
+    def _():
+        pl.semaphore_signal(barrier, inc=1, device_id={"expert": e - 2}, device_id_type=MESH)
+
+    @pl.when(z < chips - 1)
+    def _():
+        pl.semaphore_signal(barrier, inc=1, device_id={"expert": e + 2}, device_id_type=MESH)
+
+    mine = pl.ds(pl.multiple_of(c * rows, rows), rows)
+    tok = x_buf.at[z, d, mine]
+    tok_load = pltpu.make_async_copy(tok_hbm, tok, i_sem.at[0])
+    ids_load = pltpu.make_async_copy(ids_hbm, ids, i_sem.at[1])
+    levels_load = pltpu.make_async_copy(levels_hbm, levels, i_sem.at[2])
+    for load in (tok_load, ids_load, levels_load):
+        load.start()
     loads = []
     for x in range(exp_dev):
         for i, (source, held) in enumerate(((gate_hbm, gate_w), (up_hbm, up_w))):
@@ -94,23 +121,9 @@
     for load in loads:
         load.start()
 
-    barrier = pltpu.get_barrier_semaphore()
-    pl.semaphore_signal(barrier, inc=1, device_id={"dp": 1 - d}, device_id_type=MESH)
-    pl.semaphore_signal(barrier, inc=1, device_id={"expert": mate}, device_id_type=MESH)
-    for i in range(1, chips):
-        pl.semaphore_signal(
-            barrier, inc=1, device_id={"expert": lax.rem(z + i, chips) * 2 + c}, device_id_type=MESH
-        )
-
-    own_rows = pl.ds(pl.multiple_of(c * rows, rows), rows)
-    lane = lax.broadcasted_iota(jnp.int32, (rows, 128), 1)
-    share = jnp.zeros((rows, 128), jnp.float32)
-    for k in range(ids.shape[1]):
-        level = levels[:, k : k + 1].astype(jnp.float32) / 256.0
-        share = share + jnp.where(ids[:, k : k + 1] == lane, level, 0.0)
-    s_buf[z, own_rows, :] = share.astype(s_buf.dtype)
-    x_buf[z, d, own_rows, :] = tok[...]
-    pl.semaphore_wait(barrier, chips + 1)
+    pl.semaphore_wait(barrier, 2 + jnp.minimum(z, 1) + jnp.minimum(chips - 1 - z, 1))
+
+    tok_load.wait()
 
     def unit(q, core, j):
         at = pl.ds(pl.multiple_of(core * rows, rows), rows)
@@ -171,11 +184,19 @@
 
     swap().start()
     send_own(d)
+    ids_load.wait()
+    levels_load.wait()
+    label = lax.broadcasted_iota(jnp.int32, (128, rows), 0)
+    share = jnp.zeros((128, rows), jnp.float32)
+    for k in range(ids.shape[0]):
+        level = levels[k : k + 1, :].astype(jnp.float32) / 256.0
+        share = share + jnp.where(ids[k : k + 1, :] == label, level, 0.0)
+    s_buf[z, mine, :] = share.T.astype(s_buf.dtype)
     send_own(2)
     arrived(z, c, 1 - d)
     send_own(1 - d)
 
-    table = near_first(chips)
+    table = visit_order(chips)
     order = []
     for step in range(chips):
         q = jnp.int32(0)
@@ -183,17 +204,20 @@
             q = jnp.where(z == place, jnp.int32(table[place][step]), q)
         order.append(q)
 
-    def cross(step, x):
+    def piece_of(step, x, side, t):
+        return hid.at[step, x, side, :, pl.ds(pl.multiple_of(t * WIDE, WIDE), WIDE)]
+
+    def cross(step, x, t):
         return pltpu.make_async_remote_copy(
-            src_ref=hid.at[step, x, d], dst_ref=hid.at[step, x, d],
-            send_sem=h_send.at[step, x], recv_sem=h_recv.at[step, x],
+            src_ref=piece_of(step, x, d, t), dst_ref=piece_of(step, x, d, t),
+            send_sem=h_send.at[step, x, t], recv_sem=h_recv.at[step, x, t],
             device_id={"dp": 1 - d}, device_id_type=MESH,
         )
 
-    def crossed(step, x):
+    def crossed(step, x, t):
         pltpu.make_async_remote_copy(
-            src_ref=hid.at[step, x, 1 - d], dst_ref=hid.at[step, x, 1 - d],
-            send_sem=h_send.at[step, x], recv_sem=h_recv.at[step, x],
+            src_ref=piece_of(step, x, 1 - d, t), dst_ref=piece_of(step, x, 1 - d, t),
+            send_sem=h_send.at[step, x, t], recv_sem=h_recv.at[step, x, t],
             device_id={"dp": 1 - d}, device_id_type=MESH,
         ).wait_recv()
 
@@ -215,20 +239,20 @@
                 up = jnp.dot(low, up_w[x, :half, cols], preferred_element_type=jnp.float32)
                 up = up + jnp.dot(high, up_w[x, half:, cols], preferred_element_type=jnp.float32)
                 hid[step, x, d, :, cols] = (gate / (1.0 + jnp.exp(-gate)) * up).astype(hid.dtype)
-
-            cross(step, x).start()
-
-    def hand_over(step):
+                cross(step, x, t).start()
+
+
+    def hand_over(step, t):
         return pltpu.make_async_remote_copy(
-            src_ref=pair_out.at[step], dst_ref=pair_in.at[step],
-            send_sem=p_send.at[step], recv_sem=p_recv.at[step],
+            src_ref=pair_out.at[step, t], dst_ref=pair_in.at[step, t],
+            send_sem=p_send.at[step, t], recv_sem=p_recv.at[step, t],
             device_id={"expert": mate}, device_id_type=MESH,
         )
 
-    def give_back(step):
+    def give_back(step, t):
         return pltpu.make_async_remote_copy(
-            src_ref=ret_out.at[step], dst_ref=ret_in.at[z],
-            send_sem=r_send.at[step], recv_sem=r_recv.at[z],
+            src_ref=ret_out.at[step, t], dst_ref=ret_in.at[z, t],
+            send_sem=r_send.at[step, t], recv_sem=r_recv.at[z, t],
             device_id={"expert": order[step] * 2 + c}, device_id_type=MESH,
         )
 
@@ -240,7 +264,8 @@
                 loads[2 * exp_dev + x].wait()
             picked = jnp.where(lanes == e * exp_dev + x, s_buf[q].astype(jnp.float32), 0.0)
             weight = jnp.sum(picked, axis=1, keepdims=True)
-            crossed(step, x)
+            for t in range(ff // WIDE):
+                crossed(step, x, t)
 
             @pl.loop(0, width // WIDE)
             def _(t):
@@ -251,48 +276,63 @@
                 for core in range(2):
                     piece = res[core * rows : (core + 1) * rows]
                     if x == 0:
-                        part[core, :, cols] = piece
+                        part[t, core] = piece
                     else:
-                        part[core, :, cols] += piece
-
-        pair_out[step] = part[1 - c].astype(pair_out.dtype)
-        hand_over(step).start()
-        hand_over(step).wait_recv()
-        both = part[c] + pair_in[step].astype(jnp.float32)
-        if step == 0:
-            total[...] = both
-        else:
-            ret_out[step] = both.astype(ret_out.dtype)
-            give_back(step).start()
-
-    units(0)
-    for step in range(1, chips):
-        relay(step)
+                        part[t, core] += piece
+                if x == exp_dev - 1:
+                    pair_out[step, t] = part[t, 1 - c].astype(pair_out.dtype)
+                    hand_over(step, t).start()
+
+        for t in range(width // WIDE):
+            hand_over(step, t).wait_recv()
+            both = part[t, c] + pair_in[step, t].astype(jnp.float32)
+            if step == 0:
+                total[t] = both
+            else:
+                ret_out[step, t] = both.astype(ret_out.dtype)
+                give_back(step, t).start()
+
+    relayed = 0
+    for step in range(chips):
+        needed = max(abs(table[place][step] - place) for place in range(chips))
+        while relayed < needed:
+            relayed += 1
+            relay(relayed)
         units(step)
-        outputs(step - 1)
+        if step >= 1:
+            if relayed + 1 < chips - 1:
+                relayed += 1
+                relay(relayed)
+            outputs(step - 1)
     outputs(chips - 1)
 
     for i in range(1, chips):
         q = lax.rem(z + i, chips)
-        pltpu.make_async_remote_copy(
-            src_ref=ret_in.at[q], dst_ref=ret_in.at[q], send_sem=r_send.at[i], recv_sem=r_recv.at[q],
-            device_id={"expert": mate}, device_id_type=MESH,
-        ).wait_recv()
-        if i < chips - 1:
-            total[...] += ret_in[q].astype(jnp.float32)
-        else:
-            out[...] = (total[...] + ret_in[q].astype(jnp.float32)).astype(out.dtype)
+        for t in range(width // WIDE):
+            pltpu.make_async_remote_copy(
+                src_ref=ret_in.at[q, t], dst_ref=ret_in.at[q, t],
+                send_sem=r_send.at[i, t], recv_sem=r_recv.at[q, t],
+                device_id={"expert": mate}, device_id_type=MESH,
+            ).wait_recv()
+    for t in range(width // WIDE):
+        full = total[t]
+        for i in range(1, chips):
+            full = full + ret_in[lax.rem(z + i, chips), t].astype(jnp.float32)
+        out[:, t * WIDE : (t + 1) * WIDE] = full.astype(out.dtype)
 
     swap().wait_send()
     for j in (0, 1, 2):
         send_own(j, finish=True)
     for step in range(1, chips):
         relay(step, finish=True)
-        give_back(step).wait_send()
+        for t in range(width // WIDE):
+            give_back(step, t).wait_send()
     for step in range(chips):
-        hand_over(step).wait_send()
+        for t in range(width // WIDE):
+            hand_over(step, t).wait_send()
         for x in range(exp_dev):
-            cross(step, x).wait_send()
+            for t in range(ff // WIDE):
+                cross(step, x, t).wait_send()
 
 
 def dense_on_device(tokens, expert_ids, gate_levels, gate_weight, up_weight, down_weight):
@@ -301,6 +341,8 @@
     exp_dev, depth, ff = gate_weight.shape
     width = down_weight.shape[2]
     kind = tokens.dtype
+    tiles = width // WIDE
+    picks = expert_ids.shape[1]
     vmem = pl.BlockSpec(memory_space=pltpu.VMEM)
     anywhere = pl.BlockSpec(memory_space=pl.ANY)
     dma = pltpu.SemaphoreType.DMA
@@ -308,39 +350,42 @@
     return pl.pallas_call(
         functools.partial(dense_kernel, chips),
         out_shape=jax.ShapeDtypeStruct((rows, width), kind),
-        in_specs=[vmem, vmem, vmem, anywhere, anywhere, anywhere],
+        in_specs=[anywhere] * 6,
         out_specs=vmem,
         scratch_shapes=[
+            pltpu.VMEM((picks, rows), jnp.int32),
+            pltpu.VMEM((picks, rows), jnp.int32),
             pltpu.VMEM(gate_weight.shape, kind),
             pltpu.VMEM(up_weight.shape, kind),
             pltpu.VMEM(down_weight.shape, kind),
             pltpu.VMEM((chips, 2, 2 * rows, own), kind),
             pltpu.VMEM((chips, 2 * rows, 128), kind),
             pltpu.VMEM((chips, exp_dev, 2, 2 * rows, ff), kind),
-            pltpu.VMEM((2, rows, width), jnp.float32),
-            pltpu.VMEM((chips, rows, width), kind),
-            pltpu.VMEM((chips, rows, width), kind),
-            pltpu.VMEM((chips, rows, width), kind),
-            pltpu.VMEM((chips, rows, width), kind),
-            pltpu.VMEM((rows, width), jnp.float32),
+            pltpu.VMEM((tiles, 2, rows, WIDE), jnp.float32),
+            pltpu.VMEM((chips, tiles, rows, WIDE), kind),
+            pltpu.VMEM((chips, tiles, rows, WIDE), kind),
+            pltpu.VMEM((chips, tiles, rows, WIDE), kind),
+            pltpu.VMEM((chips, tiles, rows, WIDE), kind),
+            pltpu.VMEM((tiles, rows, WIDE), jnp.float32),
+            dma((3,)),
             dma((exp_dev, 3)),
             dma((chips, 3, 3)),
             dma((chips, 2, 3)),
             dma,
-            dma((chips, exp_dev)),
-            dma((chips, exp_dev)),
-            dma((chips,)),
-            dma((chips,)),
-            dma((chips,)),
-            dma((chips,)),
+            dma((chips, exp_dev, ff // WIDE)),
+            dma((chips, exp_dev, ff // WIDE)),
+            dma((chips, tiles)),
+            dma((chips, tiles)),
+            dma((chips, tiles)),
+            dma((chips, tiles)),
         ],
         compiler_params=pltpu.CompilerParams(
-            collective_id=0, has_side_effects=True, vmem_limit_bytes=60 * 1024 * 1024
+            collective_id=0, has_side_effects=True, vmem_limit_bytes=67043328
         ),
         cost_estimate=pl.CostEstimate(
             flops=flops, bytes_accessed=2 * 3 * gate_weight.size, transcendentals=0
         ),
-    )(tokens, expert_ids, gate_levels, gate_weight, up_weight, down_weight)
+    )(tokens, expert_ids.T, gate_levels.T, gate_weight, up_weight, down_weight)
 
 
 def on_device(tokens, expert_ids, gate_levels, gate_weight, up_weight, down_weight):
@@ -353,7 +398,7 @@
         2 * rows * expert_ids.shape[1] >= rows * experts
         and lax.axis_size("dp") == 2
         and n_expert % 2 == 0
-        and n_expert >= 4
+        and n_expert >= 6
         and experts <= 128
         and rows % 16 == 0
         and own % 128 == 0

time: 63.1 us -> 57.6 us (0.913)
  Pallas kernels: 58.5 us -> 55.2 us
  local copies, waits for them, and re-layouts: 4.32 us -> 1.57 us
    pallas_call x1, Pallas kernels: 58.5 us -> 55.2 us  [dense_on_device(): pl.pallas_call(functools.partial(dense_kernel, chips), out_shape=jax.Shap...]
    unnamed x3 -> x1, local copies, waits for them, and re-layouts: 4.32 us -> 1.57 us
where the time goes in v2:
time: 57.6 us; the launch traced here: 56.8 us
  Pallas kernels  55.2 us (96%)
  local copies, waits for them, and re-layouts  1.57 us (3%)
    pallas_call x1, Pallas kernels, dense_on_device(): pl.pallas_call(functools.partial(dense_kernel, chips), out_shape=jax.Shap...  55.2 us
    unnamed x1, local copies, waits for them, and re-layouts  1.57 us

profile of v2, /device:TPU:0, one launch (start us, length us, event | category | flops | bytes accessed | tf_op | source)
XLA Modules:
  0.0 56.8 jit_solution(3683385169000640932)
XLA Ops:
  0.0 55.2 %shard_map.64 = bf16[64,1024]{1,0:T(8,128)(2,1)} custom-call(bf16[64,1024]{1,0:T(8,128)(2,1)} %tok_hbm.1, s32[8,64]{1,0:T(8,128)} %bitcast.2, s32[8,64]{1,0:T(8,128)} %bitcast.3, bf16[2,2048,768]{2,1,0:T(8,128)(2,1)} %gate_hbm.1, bf16[2,2048,768]{2,1,0:T(8,128)(2,1)} %up_hbm.1, bf16[2,1536,1024]{2,1,0:T(8,128)(2,1)} %down_hbm.1), custom_call_target="tpu_custom_call" | custom-call | flops 9663676416 | bytes 18874368 | tf_op jit(solution)/shard_map/pallas_call | solution.py:350
  55.2 1.6 %copy.8 = bf16[64,1024]{1,0:T(8,128)(2,1)} copy(bf16[64,1024]{1,0:T(8,128)(2,1)} %shard_map.64) | data formatting | bytes 262144
